TPU v7x, 32 devices: a whole 2x2x4 slice. The times are simulated.
32 devices in a mesh: dp: 8 (over z, y), tensor: 4 (over x, core).
Axes of the slice: x: 2, y: 2, z: 4, core: 2. Of those that a mesh axis runs over, the one named last changes fastest.
Arguments:
- patches: bfloat16 [8192, 1280], P('dp'), may hold values from -27 to 27
- norm_gain: float32 [1280], replicated, may hold values from 0.1 to 1.9
- norm_bias: float32 [1280], replicated, may hold values from -3 to 3
- first_weight: bfloat16 [5120, 5120], P(None, 'tensor'), may hold values from -0.078125 to 0.078125
- first_bias: float32 [5120], P('tensor'), may hold values from -3 to 3
- second_weight: bfloat16 [5120, 8192], P('tensor', 'dp'), may hold values from -0.078125 to 0.078125
- second_bias: float32 [8192], P('tensor'), may hold values from -2 to 2
- text_embeds: bfloat16 [4096, 8192], P('dp', 'tensor'), may hold values from -36 to 36
- final_gain: float32 [8192], P('tensor'), may hold values from 0.1 to 1.9
- image_grids: int32 [8, 4, 2], replicated, may hold values from 2 to 8, as said below
- routing: int32 [8, 4], replicated, may hold values from 0 to 3, each once within a row
Outputs:
- embeddings: bfloat16 [4096, 8192], P('dp', 'tensor')
- normed: bfloat16 [4096, 8192], P('dp', 'tensor')
Inputs may be any that keep to these rules, and one draw needn't show every extreme that they name: `image_grids`: each image is a grid of 3 to 8 rows by 2 to 8 columns of merged tokens; in every draw some image is 8 by 8. `routing`: each row names every offset 0 to 3 once.
All inputs are finite; a program needn't handle non-finite values.
Results may differ from a plain program's by a relative error of at most 0.006.
Values may be sent and summed in bfloat16 or wider, within the bound.
A program may use at most 128 MiB of HBM per device.

v0:
```python
import jax
import jax.numpy as jnp
from jax import lax
from jax.sharding import PartitionSpec as P

D = 8192


def passed_along(block, axis, distance):
    devices = range(lax.axis_size(axis))
    route = [((i - distance) % len(devices), i) for i in devices]
    return lax.ppermute(block, axis, route)


def per_device(
    patches,
    norm_gain,
    norm_bias,
    first_weight,
    first_bias,
    second_weight,
    second_bias,
    text_embeds,
    final_gain,
    image_grids,
    routing,
):
    patch_values = patches.astype(jnp.float32)
    centered = patch_values - jnp.mean(patch_values, axis=-1, keepdims=True)
    variance = jnp.mean(centered * centered, axis=-1, keepdims=True)
    normed_patches = centered * lax.rsqrt(variance + 1e-06) * norm_gain + norm_bias
    merged = normed_patches.reshape(-1, first_weight.shape[0]).astype(jnp.bfloat16)
    hidden = jax.nn.gelu(
        jnp.dot(merged, first_weight, preferred_element_type=jnp.float32) + first_bias,
        approximate=False,
    ).astype(jnp.bfloat16)
    own_index = lax.axis_index("dp")
    shard_count = lax.axis_size("dp")
    partial_value = jnp.dot(
        lax.all_gather(hidden, "dp", axis=0, tiled=True),
        second_weight,
        preferred_element_type=jnp.float32,
    ).astype(jnp.bfloat16)
    columns = lax.all_to_all(partial_value, "dp", split_axis=0, concat_axis=1, tiled=True)
    partial_terms = columns.astype(jnp.float32)
    summed = lax.psum_scatter(
        partial_terms.astype(jnp.bfloat16), "tensor", scatter_dimension=1, tiled=True
    ).astype(jnp.float32)
    projected = (summed + second_bias).astype(jnp.bfloat16)
    block_total = image_grids.shape[1]
    cap_rows = projected.shape[0] // block_total
    feature_width = projected.shape[1]
    block_rows = projected.reshape(block_total, cap_rows, feature_width)
    counts_all = image_grids[:, :, 0] * image_grids[:, :, 1]
    slot_ids = jnp.arange(block_total, dtype=jnp.int32)
    own_routing = lax.dynamic_index_in_dim(routing, own_index, 0, keepdims=False)
    seq_rows = text_embeds.shape[0]
    image_rows = jnp.zeros((seq_rows, feature_width), jnp.bfloat16)
    filled_rows = jnp.zeros((), jnp.int32)
    zero_index = jnp.zeros((), jnp.int32)
    for stride in range(block_total):
        own_block = jnp.sum(jnp.where(own_routing == stride, slot_ids, 0))
        outgoing = lax.dynamic_index_in_dim(block_rows, own_block, 0, keepdims=False)
        if stride > 0:
            incoming = passed_along(outgoing, "dp", stride)
        else:
            incoming = outgoing
        source_shard = (own_index - stride) % shard_count
        source_routing = lax.dynamic_index_in_dim(routing, source_shard, 0, keepdims=False)
        source_block = jnp.sum(jnp.where(source_routing == stride, slot_ids, 0))
        source_counts = lax.dynamic_index_in_dim(counts_all, source_shard, 0, keepdims=False)
        image_count = lax.dynamic_index_in_dim(source_counts, source_block, 0, keepdims=False)
        image_rows = lax.dynamic_update_slice(image_rows, incoming, (filled_rows, zero_index))
        filled_rows = filled_rows + image_count
    position = jnp.arange(seq_rows, dtype=jnp.int32)[:, None]
    embeddings = jnp.where(position < filled_rows, image_rows, text_embeds)
    embed_values = embeddings.astype(jnp.float32)
    square_total = lax.psum(jnp.sum(embed_values * embed_values, axis=-1), "tensor")
    scale_rows = lax.rsqrt(square_total / D + 1e-06)
    normed = (embed_values * scale_rows[:, None] * final_gain).astype(jnp.bfloat16)
    return (embeddings, normed)


def solution(mesh):
    placed = (
        P("dp", None),
        P(),
        P(),
        P(None, "tensor"),
        P("tensor"),
        P("tensor", "dp"),
        P("tensor"),
        P("dp", "tensor"),
        P("tensor"),
        P(),
        P(),
    )
    return jax.shard_map(
        per_device,
        mesh=mesh,
        in_specs=placed,
        out_specs=(P("dp", "tensor"), P("dp", "tensor")),
        check_vma=False,
    )
```

profile of v0, /device:TPU:0, one launch (start us, length us, event | category | flops | bytes accessed | tf_op | source)
XLA Modules:
  0.0 334.0 jit_solution(4629358095571909499)
XLA Ops:
  7.2 0.0 copy-start
  7.2 0.0 all-gather.2.cloned.1.call-start
  7.2 0.0 copy-start.1
  7.2 2.3 convert_reduce_fusion
  9.6 0.3 copy-done.1
  9.9 0.0 copy-start.3
  9.9 0.0 copy-start.4
  9.9 0.8 fusion.2
  10.7 0.0 copy-done.3
  10.8 0.0 copy-done.4
  10.8 2.5 fusion.5
  13.3 0.0 copy-start.8
  13.3 5.2 %convert_element_type.31 = bf16[256,5120]{1,0:T(8,128)(2,1)} reshape(bf16[1024,1280]{1,0:T(8,128)(2,1)} %fusion.5) | data formatting | bytes 5242880 | tf_op jit(solution)/shard_map/convert_element_type | solution.py:32
  18.5 0.0 copy-done.8
  18.5 12.5 %fusion.11 = bf16[256,1280]{1,0:T(8,128)(2,1)} fusion(bf16[256,5120]{1,0:T(8,128)(2,1)} %convert_element_type.31, bf16[5120,1280]{1,0:T(8,128)(2,1)} %param.14, f32[1280]{0:T(1024)S(1)} %copy-done.8), kind=kOutput, calls=%fused_computation.20 | convolution fusion | flops 3377070080 | bytes 16389120 | tf_op jit(solution)/shard_map/dot_general | solution.py:34
  31.1 0.0 all-gather.2.cloned.1.call-update
  31.1 0.0 reduce-scatter.2.cloned.1.call-start
  31.1 88.7 %all-gather.2.cloned.1.call-done = bf16[2048,1280]{1,0:T(8,128)(2,1)} async-done(((bf16[256,1280]{1,0:T(8,128)(2,1)}), bf16[2048,1280]{1,0:T(8,128)(2,1)}) %all-gather.2.cloned.1.call-update) | async-done | bytes 5242896 | tf_op jit(solution)/shard_map/all_gather | solution.py:40
  119.8 0.0 copy-done
  119.8 9.7 %convolution_convert_fusion = bf16[2048,1024]{1,0:T(8,128)(2,1)} fusion(bf16[2048,1280]{1,0:T(8,128)(2,1)} %all-gather.2.cloned.1.call-done, bf16[1280,1024]{1,0:T(8,128)(2,1)S(1)} %copy-done), kind=kOutput, calls=%fused_computation.13 | convolution fusion | flops 5370806272 | bytes 12058624 | tf_op jit(solution)/shard_map/dot_general | solution.py:39
  129.5 6.4 %copy.18 = bf16[8,256,1024]{1,2,0:T(8,128)(2,1)} copy(bf16[8,256,1024]{2,1,0:T(8,128)(2,1)} %bitcast.23) | data formatting | bytes 8388608 | tf_op jit(solution)/shard_map/all_to_all | solution.py:44
  136.0 96.4 %all_to_all.19 = bf16[8,256,1024]{1,2,0:T(8,128)(2,1)} all-to-all(bf16[8,256,1024]{1,2,0:T(8,128)(2,1)} %copy.18), channel_id=1, replica_groups=mesh['dp'=8,'tensor'=4] {'dp'}, dimensions={0} | all-to-all | bytes 8388608 | tf_op jit(solution)/shard_map/all_to_all | solution.py:44
  232.4 0.0 copy-start.2
  232.4 0.0 copy-start.5
  232.4 0.0 reduce-scatter.2.cloned.1.call-update
  232.5 0.6 copy-done.2
  233.0 0.3 fusion.23
  233.3 0.6 select_reduce_fusion
  236.6 0.7 select_reduce_fusion.2
  239.8 0.7 select_reduce_fusion.4
  243.1 0.7 select_reduce_fusion.6
  251.3 24.8 %reduce-scatter.2.cloned.1.call-done = bf16[256,2048]{0,1:T(8,128)(2,1)} async-done(((bf16[256,8192]{0,1:T(8,128)(2,1)}), bf16[256,2048]{0,1:T(8,128)(2,1)}) %reduce-scatter.2.cloned.1.call-update) | async-done | bytes 1048592 | tf_op jit(solution)/shard_map/reduce_scatter | solution.py:46
  276.1 0.0 copy-done.5
  276.1 2.5 add_convert_fusion
  278.6 2.3 copy.19
  280.9 0.0 copy-start.7
  280.9 2.0 dynamic-slice_bitcast_fusion
  282.9 1.4 collective-permute-start
  284.3 1.5 collective-permute-start.1
  285.8 2.4 collective-permute-start.2
  288.2 0.0 copy-done.7
  288.2 0.7 constant_dynamic-slice_fusion.1
  293.1 1.6 dynamic_update_slice.12
  294.7 0.5 collective-permute-done
  295.2 2.8 dynamic_update_slice.13
  298.0 0.0 collective-permute-done.1
  298.0 2.8 dynamic_update_slice.14
  300.8 9.9 %collective-permute-done.2 = bf16[64,2048]{1,0:T(8,128)(2,1)} collective-permute-done((bf16[64,2048]{1,0:T(8,128)(2,1)S(1)}, bf16[64,2048]{1,0:T(8,128)(2,1)}, u32[]{:S(2)}, u32[]{:S(2)}) %collective-permute-start.2) | collective-permute-done | bytes 262176 | tf_op jit(solution)/shard_map/ppermute | solution.py:12
  310.6 2.8 dynamic_update_slice.15
  313.4 0.0 copy-start.6
  313.4 4.4 %fusion.6 = (f32[512]{0:T(512)S(1)}, bf16[512,2048]{1,0:T(8,128)(2,1)}) fusion(bf16[512,2048]{1,0:T(8,128)(2,1)} %dynamic_update_slice.15, bf16[512,2048]{1,0:T(8,128)(2,1)} %param.18, pred[512]{0:T(512)(128)(4,1)S(1)} %iota_compare_fusion), kind=kLoop, calls=%fused_computation.10 | loop fusion | flops 4193792 | bytes 6294016 | tf_op jit(solution)/shard_map/reduce_sum | solution.py:78
  317.8 5.9 %psum.7 = f32[512]{0:T(512)S(1)} all-reduce(f32[512]{0:T(512)S(1)} %get-tuple-element.10), channel_id=1, replica_groups=mesh['dp'=8,'tensor'=4] {'tensor'}, use_global_device_ids=true, to_apply=%region_12.13 | all-reduce | flops 512 | bytes 4096 | tf_op jit(solution)/shard_map/psum | solution.py:78
  323.7 0.0 copy-done.6
  323.7 3.5 %fusion.8 = bf16[512,2048]{1,0:T(8,128)(2,1)} fusion(bf16[512,2048]{1,0:T(8,128)(2,1)} %get-tuple-element.11, f32[2048]{0:T(1024)S(1)} %copy-done.6, f32[512]{0:T(512)S(1)} %add_rsqrt_fusion.1), kind=kLoop, calls=%fused_computation.12 | loop fusion | flops 4194304 | bytes 4204544 | tf_op jit(solution)/shard_map/convert_element_type | solution.py:80
  (5 shorter events, 0.0 us)
Async XLA Ops:
  7.2 112.7 %copy-start = (bf16[1280,1024]{1,0:T(8,128)(2,1)S(1)}, bf16[1280,1024]{1,0:T(8,128)(2,1)}, u32[]{:S(2)}) copy-start(bf16[1280,1024]{1,0:T(8,128)(2,1)} %param.16) | copy-start | bytes 7864324
  7.2 112.7 %all-gather.2.cloned.1.call-start = ((), (), s32[]{:S(2)}) async-start(), calls=%async_computation.2 | async-start | bytes 5898240 | tf_op jit(solution)/shard_map/all_gather | solution.py:40
  7.2 2.7 copy-start.1
  9.9 0.8 copy-start.3
  9.9 0.8 copy-start.4
  13.3 5.3 %copy-start.8 = (f32[1280]{0:T(1024)S(1)}, f32[1280]{0:T(1024)}, u32[]{:S(2)}) copy-start(f32[1280]{0:T(1024)} %param.15) | copy-start | bytes 15364
  31.1 245.0 %reduce-scatter.2.cloned.1.call-start = ((), (), s32[]{:S(2)}) async-start(), calls=%async_computation.3 | async-start | bytes 5242880 | tf_op jit(solution)/shard_map/reduce_scatter | solution.py:46
  232.4 0.7 copy-start.2
  232.4 43.7 %copy-start.5 = (f32[2048]{0:T(1024)S(1)}, f32[2048]{0:T(1024)}, u32[]{:S(2)}) copy-start(f32[2048]{0:T(1024)} %param.17) | copy-start | bytes 24580
  280.9 7.3 %copy-start.7 = (s32[8,4,2]{0,2,1:T(2,128)S(1)}, s32[8,4,2]{0,2,1:T(2,128)}, u32[]{:S(2)}) copy-start(s32[8,4,2]{0,2,1:T(2,128)} %param.20) | copy-start | bytes 772
  282.9 12.3 %collective-permute-start = (bf16[64,2048]{1,0:T(8,128)(2,1)}, bf16[64,2048]{1,0:T(8,128)(2,1)}, u32[]{:S(2)}, u32[]{:S(2)}) collective-permute-start(bf16[64,2048]{1,0:T(8,128)(2,1)} %get-tuple-element.14), channel_id=1, source_target_pairs={{28,0},{0,4},{4,8},{8,12},{12,16},{16,20},{20,24},{24,28},{29,1},{... | collective-permute-start | bytes 786440 | tf_op jit(solution)/shard_map/ppermute | solution.py:12
  284.3 13.7 %collective-permute-start.1 = (bf16[64,2048]{1,0:T(8,128)(2,1)S(1)}, bf16[64,2048]{1,0:T(8,128)(2,1)}, u32[]{:S(2)}, u32[]{:S(2)}) collective-permute-start(bf16[64,2048]{1,0:T(8,128)(2,1)S(1)} %get-tuple-element.13), channel_id=1, source_target_pairs={{24,0},{28,4},{0,8},{4,12},{8,16},{12,20},{16,24},{20,28},{25,1},{... | collective-permute-start | bytes 786440 | tf_op jit(solution)/shard_map/ppermute | solution.py:12
  285.8 24.8 %collective-permute-start.2 = (bf16[64,2048]{1,0:T(8,128)(2,1)S(1)}, bf16[64,2048]{1,0:T(8,128)(2,1)}, u32[]{:S(2)}, u32[]{:S(2)}) collective-permute-start(bf16[64,2048]{1,0:T(8,128)(2,1)S(1)} %get-tuple-element.12), channel_id=1, source_target_pairs={{20,0},{24,4},{28,8},{0,12},{4,16},{8,20},{12,24},{16,28},{21,1},{... | collective-permute-start | bytes 786440 | tf_op jit(solution)/shard_map/ppermute | solution.py:12
  313.4 10.2 %copy-start.6 = (f32[2048]{0:T(1024)S(1)}, f32[2048]{0:T(1024)}, u32[]{:S(2)}) copy-start(f32[2048]{0:T(1024)} %param.19) | copy-start | bytes 24580
Sparse Core Ops, SparseCore 0:
  31.2 88.5 all-gather.1
  232.5 43.5 reduce-scatter.1
where the time goes:
time: 335 us; the launch traced here: 334 us
  waiting for transfers between devices  124 us (37%)
  blocking collectives  102 us (30%)
  between operations  33.7 us (10%)
  local copies, waits for them, and re-layouts  27.5 us (8%)
  matrix products  22.2 us (7%)
  other arithmetic  19.1 us (6%)
  starting transfers between devices  5.41 us (2%)
    all_to_all x1, blocking collectives, per_device(): lax.all_to_all(partial_value, 'dp', split_axis=0, concat_axis=1, tiled=True)  96.4 us
    all_gather x1, waiting for transfers between devices, per_device(): lax.all_gather(hidden, 'dp', axis=0, tiled=True)  88.7 us
    reduce_scatter x1, waiting for transfers between devices, per_device(): lax.psum_scatter(partial_terms.astype(jnp.bfloat16), 'tensor', scatter_di...  24.8 us
    dot_general x1, matrix products, per_device(): jnp.dot(merged, first_weight, preferred_element_type=jnp.float32)  12.5 us
    ppermute x3, waiting for transfers between devices, passed_along(): return lax.ppermute(block, axis, route)  10.3 us
    dynamic_update_slice x4, local copies, waits for them, and re-layouts, per_device(): lax.dynamic_update_slice(image_rows, incoming, (filled_rows, zero_index))  9.95 us
    dot_general x1, matrix products, per_device(): jnp.dot(lax.all_gather(hidden, 'dp', axis=0, tiled=True), second_weight,...  9.71 us
  transfers between devices with their start and end apart: 5, of which 4 were waited for; matrix products, arithmetic and copies ran while one was open for 3% of the time, Pallas kernels for 0%

commit v1 on v0

v1 whole, which is shorter than its diff:
```python
import jax
import jax.numpy as jnp
from jax import lax
from jax.sharding import PartitionSpec as P


def per_device(
    patches,
    norm_gain,
    norm_bias,
    first_weight,
    first_bias,
    second_weight,
    second_bias,
    text_embeds,
    final_gain,
    image_grids,
    routing,
):
    own_index = lax.axis_index("dp")
    own_group = lax.axis_index("tensor")
    shard_count = lax.axis_size("dp")
    group_count = lax.axis_size("tensor")
    block_total = image_grids.shape[1]
    slot_rows = patches.shape[0] * patches.shape[1] // first_weight.shape[0]
    cap_rows = slot_rows // block_total
    seq_rows, feature_width = text_embeds.shape
    slot_ids = jnp.arange(block_total, dtype=jnp.int32)

    chosen = jnp.argmax(routing[:, None, :] == slot_ids[None, :, None], axis=-1)
    counts = jnp.take_along_axis(image_grids[:, :, 0] * image_grids[:, :, 1], chosen, axis=1)

    patch_values = patches.astype(jnp.float32)
    centered = patch_values - jnp.mean(patch_values, axis=-1, keepdims=True)
    variance = jnp.mean(centered * centered, axis=-1, keepdims=True)
    normed_patches = centered * lax.rsqrt(variance + 1e-06) * norm_gain + norm_bias
    merged = normed_patches.reshape(-1, first_weight.shape[0]).astype(jnp.bfloat16)
    hidden = jax.nn.gelu(
        jnp.dot(merged, first_weight, preferred_element_type=jnp.float32) + first_bias,
        approximate=False,
    ).astype(jnp.bfloat16)
    own_chosen = lax.dynamic_index_in_dim(chosen, own_index, 0, keepdims=False)
    hidden_blocks = hidden.reshape(block_total, cap_rows, -1)
    hidden = jnp.concatenate(
        [lax.dynamic_index_in_dim(hidden_blocks, own_chosen[k], 0, keepdims=False) for k in range(block_total)], axis=0
    )
    partial_value = jnp.dot(
        lax.all_gather(hidden, "dp", axis=0, tiled=True),
        second_weight,
        preferred_element_type=jnp.float32,
    ).astype(jnp.bfloat16)
    by_stride = partial_value.reshape(shard_count, block_total, cap_rows, -1)
    pieces = by_stride.reshape(shard_count, group_count, -1, by_stride.shape[-1])
    summed = lax.psum_scatter(pieces, "tensor", scatter_dimension=1, tiled=True)
    summed = summed.reshape(shard_count, -1, pieces.shape[-1])
    own_stride = own_group * block_total // group_count
    twice = jnp.concatenate([summed, summed], axis=0)
    rolled = lax.dynamic_slice_in_dim(twice, (shard_count - own_stride) % shard_count, shard_count, 0)
    wide = lax.all_to_all(rolled, "dp", split_axis=0, concat_axis=2, tiled=True)
    wide = wide.reshape(wide.shape[1], -1)
    block_rows = lax.all_to_all(wide, "tensor", split_axis=1, concat_axis=0, tiled=True)
    block_rows = (block_rows.astype(jnp.float32) + second_bias).astype(jnp.bfloat16)
    block_rows = block_rows.reshape(block_total, cap_rows, feature_width)

    image_rows = jnp.zeros((seq_rows, feature_width), jnp.bfloat16)
    filled_rows = jnp.zeros((), jnp.int32)
    zero_index = jnp.zeros((), jnp.int32)
    for stride in range(block_total):
        source_counts = lax.dynamic_index_in_dim(counts, (own_index - stride) % shard_count, 0, keepdims=False)
        image_rows = lax.dynamic_update_slice(image_rows, block_rows[stride], (filled_rows, zero_index))
        filled_rows = filled_rows + source_counts[stride]
    position = jnp.arange(seq_rows, dtype=jnp.int32)[:, None]
    embeddings = jnp.where(position < filled_rows, image_rows, text_embeds)
    embed_values = embeddings.astype(jnp.float32)
    square_total = lax.psum(jnp.sum(embed_values * embed_values, axis=-1), "tensor")
    scale_rows = lax.rsqrt(square_total / (feature_width * group_count) + 1e-06)
    normed = (embed_values * scale_rows[:, None] * final_gain).astype(jnp.bfloat16)
    return (embeddings, normed)


def solution(mesh):
    placed = (
        P("dp", None),
        P(),
        P(),
        P(None, "tensor"),
        P("tensor"),
        P("tensor", "dp"),
        P("tensor"),
        P("dp", "tensor"),
        P("tensor"),
        P(),
        P(),
    )
    return jax.shard_map(
        per_device,
        mesh=mesh,
        in_specs=placed,
        out_specs=(P("dp", "tensor"), P("dp", "tensor")),
        check_vma=False,
    )
```

time: 335 us -> 274 us (0.82)
  blocking collectives: 102 us -> 36.7 us
  waiting for transfers between devices: 124 us -> 138 us
  between operations: 33.7 us -> 26.7 us
    all_to_all x1, blocking collectives: 96.4 us -> 30.9 us  [per_device(): wide = lax.all_to_all(rolled, 'dp', split_axis=0, concat_axis=2, tiled=True)]
    reduce_scatter x1, waiting for transfers between devices: 24.8 us -> 42.9 us  [per_device(): summed = lax.psum_scatter(pieces, 'tensor', scatter_dimension=1, tiled=True)]
    ppermute x3 -> x0, waiting for transfers between devices: 10.3 us -> none  [passed_along(): return lax.ppermute(block, axis, route)]
    all_to_all x0 -> x1, waiting for transfers between devices: none -> 6.21 us  [per_device(): lax.all_to_all(wide, 'tensor', split_axis=1, concat_axis=0, tiled=True)]
    ppermute x3 -> x0, starting transfers between devices: 5.33 us -> none  [passed_along(): return lax.ppermute(block, axis, route)]
    all_to_all x0 -> x1, starting transfers between devices: none -> 4.37 us  [per_device(): lax.all_to_all(wide, 'tensor', split_axis=1, concat_axis=0, tiled=True)]
    all_to_all x1 -> x3, local copies, waits for them, and re-layouts: 6.45 us -> 6.96 us  [the longest x2 5.41 us: per_device(): lax.all_to_all(wide, 'tensor', split_axis=1, concat_axis=0, tiled=True)]
  transfers between devices with their start and end apart: 5 -> 3, of which waited for: 4 -> 3; matrix products, arithmetic and copies ran while one was open for 3% -> 1% of each run, Pallas kernels for 0% -> 0%
where the time goes in v1:
time: 274 us; the launch traced here: 273 us
  waiting for transfers between devices  138 us (50%)
  blocking collectives  36.7 us (13%)
  local copies, waits for them, and re-layouts  28.8 us (11%)
  between operations  26.7 us (10%)
  matrix products  20 us (7%)
  other arithmetic  18.8 us (7%)
  starting transfers between devices  4.63 us (2%)
    all_gather x1, waiting for transfers between devices, per_device(): lax.all_gather(hidden, 'dp', axis=0, tiled=True)  88.5 us
    reduce_scatter x1, waiting for transfers between devices, per_device(): summed = lax.psum_scatter(pieces, 'tensor', scatter_dimension=1, tiled=True)  42.9 us
    all_to_all x1, blocking collectives, per_device(): wide = lax.all_to_all(rolled, 'dp', split_axis=0, concat_axis=2, tiled=True)  30.9 us
    dot_general x1, matrix products, per_device(): jnp.dot(merged, first_weight, preferred_element_type=jnp.float32)  11.7 us
    dynamic_update_slice x4, local copies, waits for them, and re-layouts, per_device(): lax.dynamic_update_slice(image_rows, block_rows[stride], (filled_rows, ze...  9.72 us
    dot_general x1, matrix products, per_device(): jnp.dot(lax.all_gather(hidden, 'dp', axis=0, tiled=True), second_weight,...  8.3 us
    all_to_all x1, waiting for transfers between devices, per_device(): lax.all_to_all(wide, 'tensor', split_axis=1, concat_axis=0, tiled=True)  6.21 us
    psum x1, blocking collectives, per_device(): lax.psum(jnp.sum(embed_values * embed_values, axis=-1), 'tensor')  5.73 us
  transfers between devices with their start and end apart: 3, of which 3 were waited for; matrix products, arithmetic and copies ran while one was open for 1% of the time, Pallas kernels for 0%

profile of v1, /device:TPU:0, one launch (start us, length us, event | category | flops | bytes accessed | tf_op | source)
XLA Modules:
  0.0 273.2 jit_solution(4054195974074579271)
XLA Ops:
  7.2 0.0 copy-start
  7.2 0.0 all-gather.2.cloned.1.call-start
  7.2 1.4 iota_reduce_fusion
  8.6 0.1 constant_dynamic-slice_fusion
  8.7 0.6 fusion.22
  14.4 0.0 copy-start.1
  14.4 2.3 convert_reduce_fusion
  16.7 0.2 copy-done.1
  16.9 0.0 copy-start.2
  16.9 0.0 copy-start.3
  16.9 0.8 fusion.2
  17.8 0.0 copy-done.2
  17.8 0.0 copy-done.3
  17.8 2.5 fusion.5
  20.3 0.0 copy-start.7
  20.3 5.2 %convert_element_type.35 = bf16[256,5120]{1,0:T(8,128)(2,1)} reshape(bf16[1024,1280]{1,0:T(8,128)(2,1)} %fusion.5) | data formatting | bytes 5242880 | tf_op jit(solution)/shard_map/convert_element_type | solution.py:37
  28.1 0.0 copy-done.7
  28.1 11.7 %fusion.12 = bf16[256,1280]{1,0:T(8,128)(2,1)S(1)} fusion(bf16[256,5120]{1,0:T(8,128)(2,1)} %convert_element_type.35, bf16[5120,1280]{1,0:T(8,128)(2,1)} %param.14, f32[1280]{0:T(1024)S(1)} %copy-done.7), kind=kOutput, calls=%fused_computation.24 | convolution fusion | flops 3377070080 | bytes 16389120 | tf_op jit(solution)/shard_map/dot_general | solution.py:39
  39.8 0.1 dynamic-slice_bitcast_fusion.3
  39.9 0.9 pad_maximum_fusion
  40.8 0.0 all-gather.2.cloned.1.call-update
  40.8 0.2 reduce-scatter.2.cloned.1.call-start
  41.0 88.5 %all-gather.2.cloned.1.call-done = bf16[2048,1280]{1,0:T(8,128)(2,1)} async-done(((bf16[256,1280]{1,0:T(8,128)(2,1)}), bf16[2048,1280]{1,0:T(8,128)(2,1)}) %all-gather.2.cloned.1.call-update) | async-done | bytes 5242896 | tf_op jit(solution)/shard_map/all_gather | solution.py:48
  129.6 0.0 copy-done
  129.6 8.3 %convolution_convert_fusion = bf16[2048,1024]{1,0:T(8,128)(2,1)S(1)} fusion(bf16[2048,1280]{1,0:T(8,128)(2,1)} %all-gather.2.cloned.1.call-done, bf16[1280,1024]{1,0:T(8,128)(2,1)S(1)} %copy-done), kind=kOutput, calls=%fused_computation.14 | convolution fusion | flops 5370806272 | bytes 12058624 | tf_op jit(solution)/shard_map/dot_general | solution.py:47
  137.9 2.4 copy.33
  140.2 0.0 reduce-scatter.2.cloned.1.call-update
  140.3 42.9 %reduce-scatter.2.cloned.1.call-done = bf16[8,1,64,1024]{3,2,0,1:T(8,128)(2,1)} async-done(((bf16[8,4,64,1024]{3,2,0,1:T(8,128)(2,1)}), bf16[8,1,64,1024]{3,2,0,1:T(8,128)(2,1)}) %reduce-scatter.2.cloned.1.call-update) | async-done | bytes 1048592 | tf_op jit(solution)/shard_map/reduce_scatter | solution.py:54
  183.2 1.6 fusion.20
  184.8 30.9 %all_to_all.28 = bf16[8,64,1024]{2,1,0:T(8,128)(2,1)S(1)} all-to-all(bf16[8,64,1024]{2,1,0:T(8,128)(2,1)S(1)} %fusion.20), channel_id=1, replica_groups=mesh['dp'=8,'tensor'=4] {'dp'}, dimensions={0} | all-to-all | bytes 2097152 | tf_op jit(solution)/shard_map/all_to_all | solution.py:59
  215.7 1.5 copy.34
  217.3 2.6 all_to_all.24
  219.9 2.8 %copy.35 = bf16[64,4,2048]{2,0,1:T(8,128)(2,1)} copy(bf16[64,4,2048]{2,1,0:T(4,128)(2,1)} %all_to_all.24) | data formatting | bytes 2097152 | tf_op jit(solution)/shard_map/all_to_all | solution.py:61
  222.7 0.0 copy-start.6
  222.7 4.4 %all-to-all-start.1 = ((bf16[64,4,2048]{2,0,1:T(8,128)(2,1)}), bf16[64,4,2048]{2,0,1:T(8,128)(2,1)}, u32[]{:S(2)}, u32[]{:S(2)}) async-start(bf16[64,4,2048]{2,0,1:T(8,128)(2,1)} %copy.35), calls=%async_computation.2 | async-start | bytes 2097152 | tf_op jit(solution)/shard_map/all_to_all | solution.py:61
  227.1 0.1 copy.31
  227.2 0.1 reshape.87
  227.3 0.0 copy-done.6
  227.3 0.0 copy-start.4
  227.3 0.8 gather_fusion
  228.1 0.1 reshape.90
  228.2 0.1 copy.32
  228.2 0.1 constant_dynamic-slice_fusion.1
  228.3 0.5 slice.56
  230.1 0.6 slice.57
  232.1 0.6 slice.58
  233.4 0.6 slice.59
  235.3 6.2 %all-to-all-done.1 = bf16[64,4,2048]{2,0,1:T(8,128)(2,1)} async-done(((bf16[64,4,2048]{2,0,1:T(8,128)(2,1)}), bf16[64,4,2048]{2,0,1:T(8,128)(2,1)}, u32[]{:S(2)}, u32[]{:S(2)}) %all-to-all-start.1) | async-done | bytes 1048608 | tf_op jit(solution)/shard_map/all_to_all | solution.py:61
  241.5 0.0 copy-done.4
  241.5 1.4 fusion.9
  243.0 0.1 fusion.21
  243.1 1.6 dynamic_update_slice.12
  244.6 2.7 dynamic_update_slice.13
  247.4 2.7 dynamic_update_slice.14
  250.1 2.7 dynamic_update_slice.15
  252.8 0.0 copy-start.5
  252.8 4.4 %fusion.6 = (f32[512]{0:T(512)S(1)}, bf16[512,2048]{1,0:T(8,128)(2,1)}) fusion(bf16[512,2048]{1,0:T(8,128)(2,1)} %dynamic_update_slice.15, bf16[512,2048]{1,0:T(8,128)(2,1)} %param.18, pred[512]{0:T(512)(128)(4,1)S(1)} %iota_compare_fusion.1), kind=kLoop, calls=%fused_computation.11 | loop fusion | flops 4193792 | bytes 6294016 | tf_op jit(solution)/shard_map/reduce_sum | solution.py:75
  257.2 5.7 %psum.7 = f32[512]{0:T(512)S(1)} all-reduce(f32[512]{0:T(512)S(1)} %get-tuple-element.4), channel_id=1, replica_groups=mesh['dp'=8,'tensor'=4] {'tensor'}, use_global_device_ids=true, to_apply=%region_5.6 | all-reduce | flops 512 | bytes 4096 | tf_op jit(solution)/shard_map/psum | solution.py:75
  262.9 0.0 copy-done.5
  262.9 3.5 %fusion.8 = bf16[512,2048]{1,0:T(8,128)(2,1)} fusion(bf16[512,2048]{1,0:T(8,128)(2,1)} %get-tuple-element.5, f32[2048]{0:T(1024)S(1)} %copy-done.5, f32[512]{0:T(512)S(1)} %add_rsqrt_fusion.1), kind=kLoop, calls=%fused_computation.13 | loop fusion | flops 4194304 | bytes 4204544 | tf_op jit(solution)/shard_map/convert_element_type | solution.py:77
  (7 shorter events, 0.0 us)
Async XLA Ops:
  7.2 122.4 %copy-start = (bf16[1280,1024]{1,0:T(8,128)(2,1)S(1)}, bf16[1280,1024]{1,0:T(8,128)(2,1)}, u32[]{:S(2)}) copy-start(bf16[1280,1024]{1,0:T(8,128)(2,1)} %param.16) | copy-start | bytes 7864324
  7.2 122.4 %all-gather.2.cloned.1.call-start = ((), (), s32[]{:S(2)}) async-start(), calls=%async_computation.3 | async-start | bytes 5898240 | tf_op jit(solution)/shard_map/all_gather | solution.py:48
  14.4 2.5 copy-start.1
  16.9 0.8 copy-start.2
  16.9 0.8 copy-start.3
  20.3 7.8 %copy-start.7 = (f32[1280]{0:T(1024)S(1)}, f32[1280]{0:T(1024)}, u32[]{:S(2)}) copy-start(f32[1280]{0:T(1024)} %param.15) | copy-start | bytes 15364
  40.8 142.4 %reduce-scatter.2.cloned.1.call-start = ((), (), s32[]{:S(2)}) async-start(), calls=%async_computation.4 | async-start | bytes 5242880 | tf_op jit(solution)/shard_map/reduce_scatter | solution.py:54
  222.7 4.6 %copy-start.6 = (s32[8,4,2]{0,2,1:T(2,128)S(1)}, s32[8,4,2]{0,2,1:T(2,128)}, u32[]{:S(2)}) copy-start(s32[8,4,2]{0,2,1:T(2,128)} %param.20) | copy-start | bytes 772
  222.7 18.9 %all-to-all-start.1 = ((bf16[64,4,2048]{2,0,1:T(8,128)(2,1)}), bf16[64,4,2048]{2,0,1:T(8,128)(2,1)}, u32[]{:S(2)}, u32[]{:S(2)}) async-start(bf16[64,4,2048]{2,0,1:T(8,128)(2,1)} %copy.35), calls=%async_computation.2 | async-start | bytes 2097152 | tf_op jit(solution)/shard_map/all_to_all | solution.py:61
  227.3 14.2 %copy-start.4 = (f32[2048]{0:T(1024)S(1)}, f32[2048]{0:T(1024)}, u32[]{:S(2)}) copy-start(f32[2048]{0:T(1024)} %param.17) | copy-start | bytes 24580
  252.8 10.1 %copy-start.5 = (f32[2048]{0:T(1024)S(1)}, f32[2048]{0:T(1024)}, u32[]{:S(2)}) copy-start(f32[2048]{0:T(1024)} %param.19) | copy-start | bytes 24580
Sparse Core Ops, SparseCore 0:
  40.9 88.5 all-gather.1
  140.4 42.7 reduce-scatter.1

commit v2 on v1

v2 whole, which is shorter than its diff:
```python
import functools

import jax
import jax.numpy as jnp
from jax import lax
from jax.experimental import pallas as pl
from jax.experimental.pallas import tpu as pltpu
from jax.sharding import PartitionSpec as P

VMEM_LIMIT = 56 * 1024 * 1024


def hidden_kernel(per_token, patches_ref, gain_ref, bias_ref, weight_ref, first_bias_ref, index_ref, out_ref, rows_ref, total_ref):
    step = pl.program_id(0)
    tokens = out_ref.shape[0]

    @pl.when(step == 0)
    def _():
        gain = gain_ref[...]
        bias = bias_ref[...]

        def chunk(i, carry):
            span = pl.ds(pl.multiple_of(i * 128, 128), 128)
            values = patches_ref[span, :].astype(jnp.float32)
            centered = values - jnp.mean(values, axis=-1, keepdims=True)
            variance = jnp.mean(centered * centered, axis=-1, keepdims=True)
            normed = centered * lax.rsqrt(variance + 1e-06) * gain + bias
            for c in range(normed.shape[1] // 128):
                rows_ref[c, span, :] = normed[:, c * 128:(c + 1) * 128]
            return carry

        lax.fori_loop(0, patches_ref.shape[0] // 128, chunk, 0)
        total_ref[...] = jnp.zeros_like(total_ref)

    strips = [rows_ref[c, pl.ds(step, tokens, stride=per_token), :] for c in range(rows_ref.shape[0])]
    merged = jnp.concatenate(strips, axis=1).astype(jnp.bfloat16)
    total_ref[...] += jnp.dot(merged, weight_ref[...], preferred_element_type=jnp.float32)

    @pl.when(step == per_token - 1)
    def _():
        x = total_ref[...] + first_bias_ref[...]
        hidden = (0.5 * x * (1.0 + lax.erf(x * (0.5 ** 0.5)))).astype(jnp.bfloat16)
        columns = lax.broadcasted_iota(jnp.int32, (tokens, tokens), 1)
        pick = (columns == index_ref[...]).astype(jnp.bfloat16)
        out_ref[...] = jnp.dot(pick, hidden, preferred_element_type=jnp.float32).astype(jnp.bfloat16)


def compact_hidden(patches, norm_gain, norm_bias, first_weight, first_bias, index):
    width = patches.shape[1]
    per_token = first_weight.shape[0] // width
    tokens = patches.shape[0] // per_token
    out_width = first_weight.shape[1]
    whole = lambda shape: pl.BlockSpec(shape, lambda j: (0,) * len(shape))
    return pl.pallas_call(
        functools.partial(hidden_kernel, per_token),
        grid=(per_token,),
        in_specs=[
            whole(patches.shape),
            whole((1, width)),
            whole((1, width)),
            pl.BlockSpec((width, out_width), lambda j: (j, 0)),
            whole((1, out_width)),
            whole((tokens, 1)),
        ],
        out_specs=whole((tokens, out_width)),
        out_shape=jax.ShapeDtypeStruct((tokens, out_width), jnp.bfloat16),
        scratch_shapes=[
            pltpu.VMEM((width // 128, patches.shape[0], 128), jnp.float32),
            pltpu.VMEM((tokens, out_width), jnp.float32),
        ],
        compiler_params=pltpu.CompilerParams(vmem_limit_bytes=VMEM_LIMIT),
        cost_estimate=pl.CostEstimate(
            flops=2 * tokens * first_weight.size, bytes_accessed=2 * first_weight.size, transcendentals=0
        ),
        name="compact_hidden",
    )(patches, norm_gain[None], norm_bias[None], first_weight, first_bias[None], index[:, None])


def project_kernel(strides, *refs):
    index_ref, weight_ref, out_ref = refs[strides], refs[strides + 1], refs[strides + 2]
    rows = out_ref.shape[1]
    index = index_ref[0]
    columns = lax.broadcasted_iota(jnp.int32, (rows, rows), 1)
    total = None
    for k in range(strides):
        pick = (columns + k * rows == index).astype(jnp.bfloat16)
        term = jnp.dot(pick, refs[k][0], preferred_element_type=jnp.float32)
        total = term if total is None else total + term
    out_ref[0] = jnp.dot(total.astype(jnp.bfloat16), weight_ref[...], preferred_element_type=jnp.float32).astype(jnp.bfloat16)


def project(gathered, second_weight, index, strides):
    shards, rows, depth = gathered.shape
    width = second_weight.shape[1]
    source = lambda k: pl.BlockSpec((1, rows, depth), lambda e: ((e + shards - k) % shards, 0, 0))
    return pl.pallas_call(
        functools.partial(project_kernel, strides),
        grid=(shards,),
        in_specs=[source(k) for k in range(strides)]
        + [pl.BlockSpec((1, rows, 1), lambda e: (e, 0, 0)), pl.BlockSpec((depth, width), lambda e: (0, 0))],
        out_specs=pl.BlockSpec((1, rows, width), lambda e: (e, 0, 0)),
        out_shape=jax.ShapeDtypeStruct((shards, rows, width), jnp.bfloat16),
        compiler_params=pltpu.CompilerParams(vmem_limit_bytes=VMEM_LIMIT),
        cost_estimate=pl.CostEstimate(
            flops=2 * shards * rows * depth * width, bytes_accessed=4 * gathered.size, transcendentals=0
        ),
        name="project",
    )(*([gathered] * strides), index[:, :, None], second_weight)


def per_device(
    patches,
    norm_gain,
    norm_bias,
    first_weight,
    first_bias,
    second_weight,
    second_bias,
    text_embeds,
    final_gain,
    image_grids,
    routing,
):
    own_index = lax.axis_index("dp")
    shards = lax.axis_size("dp")
    groups = lax.axis_size("tensor")
    strides = image_grids.shape[1]
    slots = patches.shape[0] * patches.shape[1] // first_weight.shape[0]
    cap = slots // strides
    seq_rows, feature_width = text_embeds.shape
    slot_ids = jnp.arange(strides, dtype=jnp.int32)
    lower = (slot_ids[:, None] < slot_ids[None, :]).astype(jnp.int32)

    is_at = (routing[:, None, :] == slot_ids[None, :, None]).astype(jnp.int32)
    areas = image_grids[:, :, 0] * image_grids[:, :, 1]
    counts = jnp.sum(is_at * areas[:, None, :], axis=-1)
    chosen = jnp.sum(is_at * slot_ids, axis=-1)
    starts = jnp.sum(counts[:, :, None] * lower, axis=1)
    arriving = jnp.stack([jnp.roll(counts[:, k], k) for k in range(strides)], axis=1)
    source_starts = jnp.stack([jnp.roll(starts[:, k], k) for k in range(strides)], axis=1)
    laid_at = jnp.sum(arriving[:, :, None] * lower, axis=1)
    filled = jnp.sum(arriving, axis=1)
    most = jnp.maximum(jnp.max(jnp.sum(counts, axis=1)), jnp.max(filled))

    position = jnp.arange(slots, dtype=jnp.int32)
    own = lambda table: lax.dynamic_index_in_dim(table, own_index, 0, keepdims=False)
    inside = position[:, None] - own(starts)[None, :]
    live = (inside >= 0) & (inside < own(counts)[None, :])
    own_pick = jnp.sum(jnp.where(live, own(chosen)[None, :] * cap + inside + 1, 0), axis=1) - 1
    hidden = compact_hidden(patches, norm_gain, norm_bias, first_weight, first_bias, own_pick)

    def image_part(rows):
        inside = position[None, :rows, None] - laid_at[:, None, :]
        live = (inside >= 0) & (inside < arriving[:, None, :])
        index = jnp.sum(
            jnp.where(live, slot_ids * rows + source_starts[:, None, :] + inside + 1, 0), axis=2
        ) - 1
        gathered = lax.all_gather(hidden[:rows], "dp", axis=0)
        partial_value = project(gathered, second_weight, index, strides)
        pieces = partial_value.reshape(shards, groups, rows // groups, -1)
        summed = lax.psum_scatter(pieces, "tensor", scatter_dimension=1, tiled=True)
        summed = summed.reshape(shards, rows // groups, -1)
        wide = lax.all_to_all(summed, "dp", split_axis=0, concat_axis=2, tiled=True)
        wide = wide.reshape(rows // groups, -1)
        image_rows = lax.all_to_all(wide, "tensor", split_axis=1, concat_axis=0, tiled=True)
        return jnp.pad(image_rows, ((0, slots - rows), (0, 0)))

    buckets = (slots * 3 // 4, slots)
    image_rows = lax.cond(
        most <= buckets[0],
        lambda: image_part(buckets[0]),
        lambda: image_part(buckets[1]),
    )
    image_rows = (image_rows.astype(jnp.float32) + second_bias).astype(jnp.bfloat16)
    image_rows = jnp.pad(image_rows, ((0, seq_rows - slots), (0, 0)))
    row_ids = jnp.arange(seq_rows, dtype=jnp.int32)[:, None]
    embeddings = jnp.where(row_ids < own(filled), image_rows, text_embeds)
    embed_values = embeddings.astype(jnp.float32)
    square_total = lax.psum(jnp.sum(embed_values * embed_values, axis=-1), "tensor")
    scale_rows = lax.rsqrt(square_total / (feature_width * groups) + 1e-06)
    normed = (embed_values * scale_rows[:, None] * final_gain).astype(jnp.bfloat16)
    return (embeddings, normed)


def solution(mesh):
    placed = (
        P("dp", None),
        P(),
        P(),
        P(None, "tensor"),
        P("tensor"),
        P("tensor", "dp"),
        P("tensor"),
        P("dp", "tensor"),
        P("tensor"),
        P(),
        P(),
    )
    return jax.shard_map(
        per_device,
        mesh=mesh,
        in_specs=placed,
        out_specs=(P("dp", "tensor"), P("dp", "tensor")),
        check_vma=False,
    )
```

time: 274 us -> 222 us (0.81)
  waiting for transfers between devices: 138 us -> 110 us
  Pallas kernels: 0 us -> 25 us
  matrix products: 20 us -> 0 us
  local copies, waits for them, and re-layouts: 28.8 us -> 16 us
  between operations: 26.7 us -> 15.5 us
  other arithmetic: 18.8 us -> 9.24 us
  blocking collectives: 36.7 us -> 45.3 us
  starting transfers between devices: 4.63 us -> 0.08 us
    pallas_call x0 -> x2, Pallas kernels: none -> 25 us  [the longest x1 13.8 us: project(): pl.pallas_call(functools.partial(project_kernel, strides), grid=(shards,)...]
    dot_general x2 -> x0, matrix products: 20 us -> none  [the longest x1 11.7 us: per_device(): jnp.dot(merged, first_weight, preferred_element_type=jnp.float32)]
    all_gather x1, waiting for transfers between devices: 88.5 us -> 73.5 us  [image_part(): gathered = lax.all_gather(hidden[:rows], 'dp', axis=0)]
    dynamic_update_slice x4 -> x0, local copies, waits for them, and re-layouts: 9.72 us -> none  [per_device(): lax.dynamic_update_slice(image_rows, block_rows[stride], (filled_rows, ze...]
    all_to_all x1 -> x2, blocking collectives: 30.9 us -> 39.5 us  [the longest x1 25.5 us: image_part(): wide = lax.all_to_all(summed, 'dp', split_axis=0, concat_axis=2, tiled=True)]
    all_to_all x1 -> x0, waiting for transfers between devices: 6.21 us -> none  [per_device(): lax.all_to_all(wide, 'tensor', split_axis=1, concat_axis=0, tiled=True)]
    reduce_scatter x1, waiting for transfers between devices: 42.9 us -> 36.7 us  [image_part(): summed = lax.psum_scatter(pieces, 'tensor', scatter_dimension=1, tiled=True)]
    all_to_all x3, local copies, waits for them, and re-layouts: 6.96 us -> 1.46 us  [the longest x2 1.02 us: image_part(): lax.all_to_all(wide, 'tensor', split_axis=1, concat_axis=0, tiled=True)]
  transfers between devices with their start and end apart: 3 -> 2, of which waited for: 3 -> 2; matrix products, arithmetic and copies ran while one was open for 1% -> 1% of each run, Pallas kernels for 0% -> 0%
where the time goes in v2:
time: 222 us; the launch traced here: 221 us
  waiting for transfers between devices  110 us (50%)
  blocking collectives  45.3 us (20%)
  Pallas kernels  25 us (11%)
  local copies, waits for them, and re-layouts  16 us (7%)
  between operations  15.5 us (7%)
  other arithmetic  9.24 us (4%)
    all_gather x1, waiting for transfers between devices, image_part(): gathered = lax.all_gather(hidden[:rows], 'dp', axis=0)  73.5 us
    reduce_scatter x1, waiting for transfers between devices, image_part(): summed = lax.psum_scatter(pieces, 'tensor', scatter_dimension=1, tiled=True)  36.7 us
    all_to_all x1, blocking collectives, image_part(): wide = lax.all_to_all(summed, 'dp', split_axis=0, concat_axis=2, tiled=True)  25.5 us
    all_to_all x1, blocking collectives, image_part(): lax.all_to_all(wide, 'tensor', split_axis=1, concat_axis=0, tiled=True)  14 us
    pallas_call x1, Pallas kernels, project(): pl.pallas_call(functools.partial(project_kernel, strides), grid=(shards,)...  13.8 us
    pallas_call x1, Pallas kernels, compact_hidden(): pl.pallas_call(functools.partial(hidden_kernel, per_token), grid=(per_tok...  11.2 us
    psum x1, blocking collectives, per_device(): lax.psum(jnp.sum(embed_values * embed_values, axis=-1), 'tensor')  5.77 us
  transfers between devices with their start and end apart: 2, of which 2 were waited for; matrix products, arithmetic and copies ran while one was open for 1% of the time, Pallas kernels for 0%

profile of v2, /device:TPU:0, one launch (start us, length us, event | category | flops | bytes accessed | tf_op | source)
XLA Modules:
  0.0 221.4 jit_solution(15219740259384458094)
XLA Ops:
  7.2 0.8 slice_multiply_fusion
  8.0 0.7 select_reduce_fusion.1
  8.7 0.6 slice.117
  9.3 0.6 reduce_max.18
  9.9 0.1 slice_bitcast_fusion.6
  10.0 0.7 fusion.19
  10.7 0.1 slice_bitcast_fusion.8
  10.8 1.4 fusion.20
  13.5 0.2 multiply_reduce_fusion.3
  13.8 0.6 dynamic_slice.14
  14.4 0.6 iota_compare_fusion.2
  15.0 0.1 multiply_reduce_fusion.2
  15.1 0.6 slice.130
  15.7 0.2 dynamic-slice_reduce_fusion.1
  15.9 0.1 select_reduce_fusion.3
  16.0 0.1 slice_bitcast_fusion.1
  16.1 0.1 add_bitcast_fusion.4
  16.2 0.1 slice_bitcast_fusion.3
  16.2 0.7 add_bitcast_fusion.2
  17.0 1.3 broadcast_in_dim.16.gain_ref
  18.3 1.3 broadcast_in_dim.17.bias_ref
  19.6 1.3 broadcast_in_dim.18.first_bias_ref
  20.8 0.1 mul.95
  20.9 0.8 copy.77.index_ref
  21.7 0.0 copy-start
  21.7 11.2 %compact_hidden.1 = bf16[256,1280]{1,0:T(8,128)(2,1)S(1)} custom-call(bf16[1024,1280]{1,0:T(8,128)(2,1)} %patches_ref.1, f32[1,1280]{1,0:T(1,128)} %broadcast_in_dim.16.gain_ref, f32[1,1280]{1,0:T(1,128)} %broadcast_in_dim.17.bias_ref, bf16[5120,1280]{1,0:T(8,128)(2,1)} %weight_ref.1, f32[1,1280]{1,0:T(1,128)} %broadcast_in_dim.18.first_bias_ref, ...), custom_call_target="tpu_custom_call" | custom-call | flops 3355443200 | bytes 13107200 | tf_op jit(solution)/shard_map/compact_hidden/pallas_call | solution.py:54
  33.0 0.0 copy-done
  33.0 0.0 copy-start.4
  33.0 171.5 %conditional.6 = (bf16[256,2048]{1,0:T(8,128)(2,1)S(1)}) conditional(s32[]{:T(128)} %convert_element_type.37, (bf16[256,1280]{1,0:T(8,128)(2,1)S(1)}, s32[256]{0:T(256)S(1)}, s32[8,4]{0,1:T(4,128)S(1)}, s32[8,4,4]{0,2,1:T(4,128)S(1)}, s32[4]{0:T(128)S(1)}, /*index=5*/s32[8,4]{0,1:T(4,128)S(1)}, bf16[1280,1024]{1,0:T(8,128)(2,1)S(1)}) %tuple.44, ...), branch_computations={%region_7.11_spmd, %region_11.15_spmd} | conditional | flops 5368775168 | bytes 65448484
  33.0 0.0 all-gather.7.cloned.1.call-start
  33.0 0.8 slice.84
  33.9 0.0 all-gather.7.cloned.1.call-update
  33.9 0.0 reduce-scatter.5.cloned.1.call-start
  34.0 0.1 broadcast_add_fusion.1
  34.0 0.1 fusion.6
  34.1 1.2 copy.73.refs_4_
  35.3 73.5 %all-gather.7.cloned.1.call-done = bf16[1536,1280]{1,0:T(8,128)(2,1)} async-done(((bf16[192,1280]{1,0:T(8,128)(2,1)}), bf16[1536,1280]{1,0:T(8,128)(2,1)}) %all-gather.7.cloned.1.call-update) | async-done | bytes 3932176 | tf_op jit(solution)/shard_map/cond/branch_1_fun/all_gather | solution.py:158
  108.8 13.8 %project.3 = bf16[8,192,1024]{2,1,0:T(8,128)(2,1)} custom-call(bf16[8,192,1280]{2,1,0:T(8,128)(2,1)} %bitcast.75, bf16[8,192,1280]{2,1,0:T(8,128)(2,1)} %bitcast.76, bf16[8,192,1280]{2,1,0:T(8,128)(2,1)} %bitcast.77, bf16[8,192,1280]{2,1,0:T(8,128)(2,1)} %bitcast.78, s32[8,192,1]{2,1,0:T(8,128)} %copy.73.refs_4_, ...), custom_call_target="tpu_custom_call" | custom-call | flops 4026531840 | bytes 7864320 | tf_op jit(solution)/shard_map/cond/branch_1_fun/project/pallas_call | solution.py:96
  122.6 4.0 %copy.74 = bf16[8,4,48,1024]{3,2,0,1:T(8,128)(2,1)} copy(bf16[8,4,48,1024]{3,2,1,0:T(8,128)(2,1)} %bitcast.80) | data formatting | bytes 6291456 | tf_op jit(solution)/shard_map/cond/branch_1_fun/reshape | solution.py:160
  126.7 0.0 reduce-scatter.5.cloned.1.call-update
  126.7 36.7 %reduce-scatter.5.cloned.1.call-done = bf16[8,1,48,1024]{3,2,0,1:T(8,128)(2,1)} async-done(((bf16[8,4,48,1024]{3,2,0,1:T(8,128)(2,1)}), bf16[8,1,48,1024]{3,2,0,1:T(8,128)(2,1)}) %reduce-scatter.5.cloned.1.call-update) | async-done | bytes 786448 | tf_op jit(solution)/shard_map/cond/branch_1_fun/reduce_scatter | solution.py:161
  163.4 25.5 %all_to_all.56 = bf16[8,48,1024]{2,1,0:T(8,128)(2,1)S(1)} all-to-all(bf16[8,48,1024]{2,1,0:T(8,128)(2,1)} %bitcast.86), channel_id=1, replica_groups=mesh['dp'=8,'tensor'=4] {'dp'}, dimensions={0} | all-to-all | bytes 1572864 | tf_op jit(solution)/shard_map/cond/branch_1_fun/all_to_all | solution.py:163
  188.9 0.4 copy.75
  189.3 0.6 all_to_all.46
  189.9 0.4 copy.76
  190.3 14.0 %all_to_all.57 = bf16[48,4,2048]{2,0,1:T(8,128)(2,1)S(1)} all-to-all(bf16[48,4,2048]{2,0,1:T(8,128)(2,1)S(1)} %copy.76), channel_id=1, replica_groups=mesh['dp'=8,'tensor'=4] {'tensor'}, dimensions={1} | all-to-all | bytes 1572864 | tf_op jit(solution)/shard_map/cond/branch_1_fun/all_to_all | solution.py:165
  204.4 0.1 pad.6
  204.5 0.0 copy-done.4
  204.5 0.0 copy-start.3
  204.5 0.2 add_convert_fusion
  204.7 1.4 copy-done.3
  206.1 0.0 copy-start.5
  206.1 0.8 fusion.8
  206.9 0.0 copy-start.1
  206.9 5.8 %psum.7 = f32[512]{0:T(512)S(1)} all-reduce(f32[512]{0:T(512)S(1)} %get-tuple-element.66), channel_id=1, replica_groups=mesh['dp'=8,'tensor'=4] {'tensor'}, use_global_device_ids=true, to_apply=%region_16.17 | all-reduce | flops 512 | bytes 4096 | tf_op jit(solution)/shard_map/psum | solution.py:179
  212.7 0.0 copy-done.5
  212.7 1.9 fusion.10
  214.6 0.0 copy-done.1
  (18 shorter events, 0.1 us)
Async XLA Ops:
  21.7 11.2 %copy-start = (bf16[1280,1024]{1,0:T(8,128)(2,1)S(1)}, bf16[1280,1024]{1,0:T(8,128)(2,1)}, u32[]{:S(2)}) copy-start(bf16[1280,1024]{1,0:T(8,128)(2,1)} %param.18) | copy-start | bytes 7864324
  33.0 171.5 %copy-start.4 = (f32[2048]{0:T(1024)S(1)}, f32[2048]{0:T(1024)}, u32[]{:S(2)}) copy-start(f32[2048]{0:T(1024)} %param.19) | copy-start | bytes 24580
  33.0 75.8 %all-gather.7.cloned.1.call-start = ((), (), s32[]{:S(2)}) async-start(), calls=%async_computation.9 | async-start | bytes 4423680 | tf_op jit(solution)/shard_map/cond/branch_1_fun/all_gather | solution.py:158
  33.9 129.5 %reduce-scatter.5.cloned.1.call-start = ((), (), s32[]{:S(2)}) async-start(), calls=%async_computation.8 | async-start | bytes 3932160 | tf_op jit(solution)/shard_map/cond/branch_1_fun/reduce_scatter | solution.py:161
  204.5 1.6 copy-start.3
  206.1 6.6 %copy-start.5 = (f32[2048]{0:T(1024)S(1)}, f32[2048]{0:T(1024)}, u32[]{:S(2)}) copy-start(f32[2048]{0:T(1024)} %param.21) | copy-start | bytes 24580
  206.9 7.7 %copy-start.1 = (bf16[512,2048]{1,0:T(8,128)(2,1)}, bf16[512,2048]{1,0:T(8,128)(2,1)S(1)}, u32[]{:S(2)}) copy-start(bf16[512,2048]{1,0:T(8,128)(2,1)S(1)} %get-tuple-element.67) | copy-start | bytes 6291460
Sparse Core Ops, SparseCore 0:
  36.6 72.2 all-gather.6
  126.8 36.5 reduce-scatter.4

commit v3 on v2

--- a/solution.py
+++ b/solution.py
@@ -108,6 +108,264 @@
     )(*([gathered] * strides), index[:, :, None], second_weight)
 
 
+def gather_kernel(own_ref, out_ref, line_send, line_recv, pair_send, pair_recv):
+    shards = out_ref.shape[0]
+    length = shards // 2
+    me = lax.axis_index("dp")
+    place, row = me // 2, me % 2
+    other = me + 1 - 2 * row
+    barrier = pltpu.get_barrier_semaphore()
+    pl.semaphore_signal(barrier, inc=1, device_id={"dp": other})
+
+    @pl.when(place > 0)
+    def _():
+        pl.semaphore_signal(barrier, inc=1, device_id={"dp": me - 2})
+
+    @pl.when(place < length - 1)
+    def _():
+        pl.semaphore_signal(barrier, inc=1, device_id={"dp": me + 2})
+
+    peers = 1 + (place > 0).astype(jnp.int32) + (place < length - 1).astype(jnp.int32)
+    pl.semaphore_wait(barrier, peers)
+
+    def line_copy(block, way, src):
+        return pltpu.make_async_remote_copy(
+            src_ref=src,
+            dst_ref=out_ref.at[2 * block + row],
+            send_sem=line_send.at[(way + 1) // 2, block],
+            recv_sem=line_recv.at[block],
+            device_id={"dp": me + 2 * way},
+        )
+
+    def pair_copy(block, src, side):
+        return pltpu.make_async_remote_copy(
+            src_ref=src,
+            dst_ref=out_ref.at[2 * block + side],
+            send_sem=pair_send.at[block],
+            recv_sem=pair_recv.at[block],
+            device_id={"dp": other},
+        )
+
+    for step in range(length):
+        for way in (1, -1):
+            block = place - way * step
+            src = own_ref if step == 0 else out_ref.at[2 * block + row]
+
+            @pl.when((block >= 0) & (block < length))
+            def _(way=way, block=block, src=src, step=step):
+                if step > 0:
+                    line_copy(block, way, src).wait_recv()
+
+                @pl.when((place + way >= 0) & (place + way < length))
+                def _():
+                    line_copy(block, way, src).start()
+
+                if step > 0 or way == 1:
+                    pair_copy(block, src, row).start()
+
+    out_ref[me] = own_ref[...]
+
+    def drain(block, carry):
+        here = out_ref.at[2 * block + row]
+        pair_copy(block, here, 1 - row).wait_recv()
+        pair_copy(block, here, row).wait_send()
+
+        @pl.when((block <= place) & (place < length - 1))
+        def _():
+            line_copy(block, 1, here).wait_send()
+
+        @pl.when((block >= place) & (place > 0))
+        def _():
+            line_copy(block, -1, here).wait_send()
+
+        return carry
+
+    lax.fori_loop(0, length, drain, 0)
+
+
+def gathered_rows(own, call_id):
+    shards = lax.axis_size("dp")
+    dma = pltpu.SemaphoreType.DMA
+    return pl.pallas_call(
+        gather_kernel,
+        in_specs=[pl.BlockSpec(memory_space=pltpu.VMEM)],
+        out_specs=pl.BlockSpec(memory_space=pltpu.VMEM),
+        out_shape=jax.ShapeDtypeStruct((shards,) + own.shape, own.dtype),
+        scratch_shapes=[dma((2, shards // 2)), dma((shards // 2,)), dma((shards // 2,)), dma((shards // 2,))],
+        compiler_params=pltpu.CompilerParams(
+            collective_id=call_id, has_side_effects=True, vmem_limit_bytes=VMEM_LIMIT
+        ),
+        name="gather_rows",
+    )(own)
+
+
+def scatter_kernel(
+    part_ref, out_ref, pair_in, cross_out, cross_in, ready, wide,
+    pair_send, pair_recv, cross_send, cross_recv, wide_send, wide_recv, out_send, out_recv,
+):
+    shards, groups = part_ref.shape[0], part_ref.shape[1]
+    per_group = shards // groups
+    me = lax.axis_index("dp")
+    group = lax.axis_index("tensor")
+    core, side = group % 2, group // 2
+    mate = 2 * side + 1 - core
+    across = group + 2 - 4 * side
+    across_mate = mate + 2 - 4 * side
+    f32 = jnp.float32
+
+    barrier = pltpu.get_barrier_semaphore()
+    for peer in (mate, across, across_mate):
+        pl.semaphore_signal(barrier, inc=1, device_id={"tensor": peer})
+
+    def greet(i, carry):
+        pl.semaphore_signal(barrier, inc=1, device_id={"dp": (me + 1 + i) % shards})
+        return carry
+
+    lax.fori_loop(0, shards - 1, greet, 0)
+    pl.semaphore_wait(barrier, shards + 2)
+
+    def pair_copy(e, slot):
+        return pltpu.make_async_remote_copy(
+            src_ref=part_ref.at[e, mate if slot == 0 else across_mate],
+            dst_ref=pair_in.at[e, slot],
+            send_sem=pair_send.at[slot, e],
+            recv_sem=pair_recv.at[slot, e],
+            device_id={"tensor": mate},
+        )
+
+    def cross_copy(e):
+        return pltpu.make_async_remote_copy(
+            src_ref=cross_out.at[e],
+            dst_ref=cross_in.at[e],
+            send_sem=cross_send.at[e],
+            recv_sem=cross_recv.at[e],
+            device_id={"tensor": across},
+        )
+
+    def wide_copy(e, source):
+        return pltpu.make_async_remote_copy(
+            src_ref=ready.at[e],
+            dst_ref=wide.at[source],
+            send_sem=wide_send.at[e],
+            recv_sem=wide_recv.at[source],
+            device_id={"dp": e},
+        )
+
+    def out_copy(source, target, sender):
+        return pltpu.make_async_remote_copy(
+            src_ref=wide.at[source],
+            dst_ref=out_ref.at[sender, source % per_group],
+            send_sem=out_send.at[source],
+            recv_sem=out_recv.at[sender, source % per_group],
+            device_id={"tensor": target},
+        )
+
+    def start_pair(i, carry):
+        e = (me + 1 + i) % shards
+        for slot in (1, 0):
+            pair_copy(e, slot).start()
+        return carry
+
+    lax.fori_loop(0, shards, start_pair, 0)
+
+    def start_cross(i, carry):
+        e = (me + 1 + i) % shards
+        pair_copy(e, 1).wait_recv()
+        cross_out[e] = (part_ref[e, across].astype(f32) + pair_in[e, 1].astype(f32)).astype(jnp.bfloat16)
+        cross_copy(e).start()
+        return carry
+
+    lax.fori_loop(0, shards, start_cross, 0)
+
+    def forward(source):
+        target = source // per_group
+
+        @pl.when(target == group)
+        def _():
+            out_ref[group, source % per_group] = wide[source]
+
+        @pl.when(target != group)
+        def _():
+            out_copy(source, target, group).start()
+
+    lag = 2
+
+    def start_wide(i, carry):
+        @pl.when(i < shards)
+        def _():
+            e = (me + 1 + i) % shards
+            pair_copy(e, 0).wait_recv()
+            cross_copy(e).wait_recv()
+            total = part_ref[e, group].astype(f32) + pair_in[e, 0].astype(f32) + cross_in[e].astype(f32)
+
+            @pl.when(i < shards - 1)
+            def _():
+                ready[e] = total.astype(jnp.bfloat16)
+                wide_copy(e, me).start()
+
+            @pl.when(i == shards - 1)
+            def _():
+                wide[me] = total.astype(jnp.bfloat16)
+                forward(me)
+
+        @pl.when((i >= lag) & (i < shards - 1 + lag))
+        def _():
+            source = (me + 2 * shards - 1 - (i - lag)) % shards
+            wide_copy(source, source).wait_recv()
+            forward(source)
+
+        return carry
+
+    lax.fori_loop(0, shards + lag - 1, start_wide, 0)
+
+    def drain(i, carry):
+        e = (me + 1 + i) % shards
+        for slot in (1, 0):
+            pair_copy(e, slot).wait_send()
+        cross_copy(e).wait_send()
+
+        @pl.when(i < shards - 1)
+        def _():
+            wide_copy(e, me).wait_send()
+
+        @pl.when(e // per_group != group)
+        def _():
+            out_copy(e, e // per_group, group).wait_send()
+
+        return carry
+
+    lax.fori_loop(0, shards, drain, 0)
+    for peer in (mate, across, across_mate):
+
+        def receive(c, carry, peer=peer):
+            out_copy(group * per_group + c, peer, peer).wait_recv()
+            return carry
+
+        lax.fori_loop(0, per_group, receive, 0)
+
+
+def scattered_rows(pieces, call_id):
+    shards, groups, rows, width = pieces.shape
+    dma = pltpu.SemaphoreType.DMA
+    block = pltpu.VMEM((shards, rows, width), jnp.bfloat16)
+    out = pl.pallas_call(
+        scatter_kernel,
+        in_specs=[pl.BlockSpec(memory_space=pltpu.VMEM)],
+        out_specs=pl.BlockSpec(memory_space=pltpu.VMEM),
+        out_shape=jax.ShapeDtypeStruct((groups, shards // groups, rows, width), jnp.bfloat16),
+        scratch_shapes=[
+            pltpu.VMEM((shards, 2, rows, width), jnp.bfloat16), block, block, block, block,
+            dma((2, shards)), dma((2, shards)), dma((shards,)), dma((shards,)),
+            dma((shards,)), dma((shards,)), dma((shards,)), dma((groups, shards // groups)),
+        ],
+        compiler_params=pltpu.CompilerParams(
+            collective_id=call_id, has_side_effects=True, vmem_limit_bytes=VMEM_LIMIT
+        ),
+        name="scatter_rows",
+    )(pieces)
+    return out.transpose(0, 2, 1, 3).reshape(groups * rows, -1)
+
+
 def per_device(
     patches,
     norm_gain,
@@ -149,27 +407,23 @@
     own_pick = jnp.sum(jnp.where(live, own(chosen)[None, :] * cap + inside + 1, 0), axis=1) - 1
     hidden = compact_hidden(patches, norm_gain, norm_bias, first_weight, first_bias, own_pick)
 
-    def image_part(rows):
+    def image_part(rows, call_id):
         inside = position[None, :rows, None] - laid_at[:, None, :]
         live = (inside >= 0) & (inside < arriving[:, None, :])
         index = jnp.sum(
             jnp.where(live, slot_ids * rows + source_starts[:, None, :] + inside + 1, 0), axis=2
         ) - 1
-        gathered = lax.all_gather(hidden[:rows], "dp", axis=0)
+        gathered = gathered_rows(hidden[:rows], 2 * call_id)
         partial_value = project(gathered, second_weight, index, strides)
         pieces = partial_value.reshape(shards, groups, rows // groups, -1)
-        summed = lax.psum_scatter(pieces, "tensor", scatter_dimension=1, tiled=True)
-        summed = summed.reshape(shards, rows // groups, -1)
-        wide = lax.all_to_all(summed, "dp", split_axis=0, concat_axis=2, tiled=True)
-        wide = wide.reshape(rows // groups, -1)
-        image_rows = lax.all_to_all(wide, "tensor", split_axis=1, concat_axis=0, tiled=True)
+        image_rows = scattered_rows(pieces, 2 * call_id + 1)
         return jnp.pad(image_rows, ((0, slots - rows), (0, 0)))
 
     buckets = (slots * 3 // 4, slots)
     image_rows = lax.cond(
         most <= buckets[0],
-        lambda: image_part(buckets[0]),
-        lambda: image_part(buckets[1]),
+        lambda: image_part(buckets[0], 0),
+        lambda: image_part(buckets[1], 1),
     )
     image_rows = (image_rows.astype(jnp.float32) + second_bias).astype(jnp.bfloat16)
     image_rows = jnp.pad(image_rows, ((0, seq_rows - slots), (0, 0)))

time: 222 us -> 145 us (0.65)
  waiting for transfers between devices: 110 us -> 0 us
  Pallas kernels: 25 us -> 115 us
  blocking collectives: 45.3 us -> 5.76 us
  between operations: 15.5 us -> 2.11 us
  local copies, waits for them, and re-layouts: 16 us -> 12.6 us
    pallas_call x0 -> x2, Pallas kernels: none -> 89.5 us  [the longest x1 52.4 us: gathered_rows(): pl.pallas_call(gather_kernel, in_specs=[pl.BlockSpec(memory_space=pltpu.V...]
    all_gather x1 -> x0, waiting for transfers between devices: 73.5 us -> none  [image_part(): gathered = lax.all_gather(hidden[:rows], 'dp', axis=0)]
    all_to_all x2 -> x0, blocking collectives: 39.5 us -> none  [the longest x1 25.5 us: image_part(): wide = lax.all_to_all(summed, 'dp', split_axis=0, concat_axis=2, tiled=True)]
    reduce_scatter x1 -> x0, waiting for transfers between devices: 36.7 us -> none  [image_part(): summed = lax.psum_scatter(pieces, 'tensor', scatter_dimension=1, tiled=True)]
    reshape x1 -> x0, local copies, waits for them, and re-layouts: 4.05 us -> none  [image_part(): pieces = partial_value.reshape(shards, groups, rows // groups, -1)]
  transfers between devices with their start and end apart: 2 -> 0, of which waited for: 2 -> 0; matrix products, arithmetic and copies ran while one was open for 1% -> 0% of each run, Pallas kernels for 0% -> 0%
where the time goes in v3:
time: 145 us; the launch traced here: 144 us
  Pallas kernels  115 us (79%)
  local copies, waits for them, and re-layouts  12.6 us (9%)
  other arithmetic  9.24 us (6%)
  blocking collectives  5.76 us (4%)
  between operations  2.11 us (1%)
    pallas_call x1, Pallas kernels, gathered_rows(): pl.pallas_call(gather_kernel, in_specs=[pl.BlockSpec(memory_space=pltpu.V...  52.4 us
    pallas_call x1, Pallas kernels, scattered_rows(): pl.pallas_call(scatter_kernel, in_specs=[pl.BlockSpec(memory_space=pltpu....  37.1 us
    pallas_call x1, Pallas kernels, project(): pl.pallas_call(functools.partial(project_kernel, strides), grid=(shards,)...  13.8 us
    pallas_call x1, Pallas kernels, compact_hidden(): pl.pallas_call(functools.partial(hidden_kernel, per_token), grid=(per_tok...  11.2 us
    psum x1, blocking collectives, per_device(): lax.psum(jnp.sum(embed_values * embed_values, axis=-1), 'tensor')  5.76 us

profile of v3, /device:TPU:0, one launch (start us, length us, event | category | flops | bytes accessed | tf_op | source)
XLA Modules:
  0.0 144.3 jit_solution(5747866244556968481)
XLA Ops:
  0.7 0.8 slice_multiply_fusion
  1.4 0.7 select_reduce_fusion.1
  2.1 0.6 slice.117
  2.7 0.6 reduce_max.18
  3.4 0.1 slice_bitcast_fusion.6
  3.4 0.7 fusion.19
  4.2 0.1 slice_bitcast_fusion.8
  4.2 1.4 fusion.20
  7.0 0.2 multiply_reduce_fusion.3
  7.2 0.6 dynamic_slice.14
  7.8 0.6 iota_compare_fusion.2
  8.5 0.1 multiply_reduce_fusion.2
  8.6 0.6 slice.130
  9.2 0.2 dynamic-slice_reduce_fusion.1
  9.3 0.1 select_reduce_fusion.3
  9.4 0.1 slice_bitcast_fusion.1
  9.5 0.1 add_bitcast_fusion.4
  9.6 0.1 slice_bitcast_fusion.3
  9.7 0.7 add_bitcast_fusion.2
  10.4 1.3 broadcast_in_dim.16.gain_ref
  11.7 1.3 broadcast_in_dim.17.bias_ref
  13.0 1.3 broadcast_in_dim.18.first_bias_ref
  14.3 0.1 mul.95
  14.4 0.8 copy.52.index_ref
  15.2 0.0 copy-start
  15.2 11.2 %compact_hidden.1 = bf16[256,1280]{1,0:T(8,128)(2,1)S(1)} custom-call(bf16[1024,1280]{1,0:T(8,128)(2,1)} %patches_ref.1, f32[1,1280]{1,0:T(1,128)} %broadcast_in_dim.16.gain_ref, f32[1,1280]{1,0:T(1,128)} %broadcast_in_dim.17.bias_ref, bf16[5120,1280]{1,0:T(8,128)(2,1)} %weight_ref.1, f32[1,1280]{1,0:T(1,128)} %broadcast_in_dim.18.first_bias_ref, ...), custom_call_target="tpu_custom_call" | custom-call | flops 3355443200 | bytes 13107200 | tf_op jit(solution)/shard_map/compact_hidden/pallas_call | solution.py:54
  26.4 0.0 copy-done
  26.4 0.0 copy-start.3
  26.4 107.8 %conditional.6 = (bf16[256,2048]{1,0:T(8,128)(2,1)S(1)}) conditional(s32[]{:T(128)} %convert_element_type.37, (bf16[256,1280]{1,0:T(8,128)(2,1)S(1)}, s32[256]{0:T(256)S(1)}, s32[8,4]{0,1:T(4,128)S(1)}, s32[8,4,4]{0,2,1:T(4,128)S(1)}, s32[4]{0:T(128)S(1)}, /*index=5*/s32[8,4]{0,1:T(4,128)S(1)}, bf16[1280,1024]{1,0:T(8,128)(2,1)S(1)}) %tuple.36, ...), branch_computations={%region_7.10_spmd, %region_10.13_spmd} | conditional | flops 5368775168 | bytes 14723512
  26.5 0.8 slice.84.own_ref
  27.3 0.1 broadcast_add_fusion.1
  27.4 0.1 fusion.6
  27.5 1.2 copy.50.refs_4_
  28.7 52.4 %gather_rows.3.refs_0_.refs_1_.refs_2_.refs_3_ = bf16[8,192,1280]{2,1,0:T(8,128)(2,1)} custom-call(bf16[192,1280]{1,0:T(8,128)(2,1)} %slice.84.own_ref), custom_call_target="tpu_custom_call" | custom-call | tf_op jit(solution)/shard_map/cond/branch_1_fun/gather_rows/pallas_call | solution.py:189
  81.1 13.8 %project.3 = bf16[8,192,1024]{2,1,0:T(8,128)(2,1)} custom-call(bf16[8,192,1280]{2,1,0:T(8,128)(2,1)} %gather_rows.3.refs_0_.refs_1_.refs_2_.refs_3_, bf16[8,192,1280]{2,1,0:T(8,128)(2,1)} %gather_rows.3.refs_0_.refs_1_.refs_2_.refs_3_, bf16[8,192,1280]{2,1,0:T(8,128)(2,1)} %gather_rows.3.refs_0_.refs_1_.refs_2_.refs_3_, ...), custom_call_target="tpu_custom_call" | custom-call | flops 4026531840 | bytes 7864320 | tf_op jit(solution)/shard_map/cond/branch_1_fun/project/pallas_call | solution.py:96
  94.9 37.1 %scatter_rows.3 = bf16[4,2,48,1024]{3,2,1,0:T(8,128)(2,1)} custom-call(bf16[8,4,48,1024]{3,2,1,0:T(8,128)(2,1)} %bitcast.60), custom_call_target="tpu_custom_call" | custom-call | tf_op jit(solution)/shard_map/cond/branch_1_fun/scatter_rows/pallas_call | solution.py:351
  132.0 1.9 %copy.51 = bf16[4,48,2,1024]{3,2,1,0:T(2,128)(2,1)S(1)} copy(bf16[4,48,2,1024]{3,1,2,0:T(8,128)(2,1)} %bitcast.66) | data formatting | bytes 1572864 | tf_op jit(solution)/shard_map/cond/branch_1_fun/transpose | solution.py:366
  133.9 0.2 copy.54
  134.1 0.1 pad.6
  134.2 0.0 copy-done.3
  134.3 0.0 copy-start.2
  134.3 0.2 add_convert_fusion
  134.5 1.4 copy-done.2
  135.9 0.0 copy-start.4
  135.9 0.8 fusion.8
  136.7 0.0 copy-start.1
  136.7 5.8 %psum.7 = f32[512]{0:T(512)S(1)} all-reduce(f32[512]{0:T(512)S(1)} %get-tuple-element.66), channel_id=1, replica_groups=mesh['dp'=8,'tensor'=4] {'tensor'}, use_global_device_ids=true, to_apply=%region_14.15 | all-reduce | flops 512 | bytes 4096 | tf_op jit(solution)/shard_map/psum | solution.py:433
  142.5 0.0 copy-done.4
  142.5 1.9 %fusion.10 = bf16[512,2048]{1,0:T(8,128)(2,1)} fusion(bf16[512,2048]{1,0:T(8,128)(2,1)S(1)} %get-tuple-element.67, f32[2048]{0:T(1024)S(1)} %copy-done.4, f32[512]{0:T(512)S(1)} %add_rsqrt_fusion), kind=kLoop, calls=%fused_computation.26 | loop fusion | flops 4194304 | bytes 4204544 | tf_op jit(solution)/shard_map/convert_element_type | solution.py:435
  144.3 0.0 copy-done.1
  (18 shorter events, 0.1 us)
Async XLA Ops:
  15.2 11.2 %copy-start = (bf16[1280,1024]{1,0:T(8,128)(2,1)S(1)}, bf16[1280,1024]{1,0:T(8,128)(2,1)}, u32[]{:S(2)}) copy-start(bf16[1280,1024]{1,0:T(8,128)(2,1)} %param.18) | copy-start | bytes 7864324
  26.4 107.8 %copy-start.3 = (f32[2048]{0:T(1024)S(1)}, f32[2048]{0:T(1024)}, u32[]{:S(2)}) copy-start(f32[2048]{0:T(1024)} %param.19) | copy-start | bytes 24580
  134.3 1.6 %copy-start.2 = (bf16[512,2048]{1,0:T(8,128)(2,1)S(1)}, bf16[512,2048]{1,0:T(8,128)(2,1)}, u32[]{:S(2)}) copy-start(bf16[512,2048]{1,0:T(8,128)(2,1)} %param.20) | copy-start | bytes 6291460
  135.9 6.6 %copy-start.4 = (f32[2048]{0:T(1024)S(1)}, f32[2048]{0:T(1024)}, u32[]{:S(2)}) copy-start(f32[2048]{0:T(1024)} %param.21) | copy-start | bytes 24580
  136.7 7.7 %copy-start.1 = (bf16[512,2048]{1,0:T(8,128)(2,1)}, bf16[512,2048]{1,0:T(8,128)(2,1)S(1)}, u32[]{:S(2)}) copy-start(bf16[512,2048]{1,0:T(8,128)(2,1)S(1)} %get-tuple-element.67) | copy-start | bytes 6291460

commit v4 on v3

--- a/solution.py
+++ b/solution.py
@@ -16,8 +16,8 @@
 
     @pl.when(step == 0)
     def _():
-        gain = gain_ref[...]
-        bias = bias_ref[...]
+        gain = gain_ref[...][None, :]
+        bias = bias_ref[...][None, :]
 
         def chunk(i, carry):
             span = pl.ds(pl.multiple_of(i * 128, 128), 128)
@@ -38,7 +38,7 @@
 
     @pl.when(step == per_token - 1)
     def _():
-        x = total_ref[...] + first_bias_ref[...]
+        x = total_ref[...] + first_bias_ref[...][None, :]
         hidden = (0.5 * x * (1.0 + lax.erf(x * (0.5 ** 0.5)))).astype(jnp.bfloat16)
         columns = lax.broadcasted_iota(jnp.int32, (tokens, tokens), 1)
         pick = (columns == index_ref[...]).astype(jnp.bfloat16)
@@ -56,10 +56,10 @@
         grid=(per_token,),
         in_specs=[
             whole(patches.shape),
-            whole((1, width)),
-            whole((1, width)),
+            whole((width,)),
+            whole((width,)),
             pl.BlockSpec((width, out_width), lambda j: (j, 0)),
-            whole((1, out_width)),
+            whole((out_width,)),
             whole((tokens, 1)),
         ],
         out_specs=whole((tokens, out_width)),
@@ -73,7 +73,7 @@
             flops=2 * tokens * first_weight.size, bytes_accessed=2 * first_weight.size, transcendentals=0
         ),
         name="compact_hidden",
-    )(patches, norm_gain[None], norm_bias[None], first_weight, first_bias[None], index[:, None])
+    )(patches, norm_gain, norm_bias, first_weight, first_bias, index[:, None])
 
 
 def project_kernel(strides, *refs):

time: 145 us -> 141 us (0.972)
  local copies, waits for them, and re-layouts: 12.6 us -> 8.75 us
    broadcast_in_dim x3 -> x0, local copies, waits for them, and re-layouts: 3.88 us -> none  [the longest x1 1.3 us: compact_hidden(): norm_gain[None]]
where the time goes in v4:
time: 141 us; the launch traced here: 140 us
  Pallas kernels  115 us (82%)
  other arithmetic  9.24 us (7%)
  local copies, waits for them, and re-layouts  8.75 us (6%)
  blocking collectives  5.76 us (4%)
  between operations  2.11 us (1%)
    pallas_call x1, Pallas kernels, gathered_rows(): pl.pallas_call(gather_kernel, in_specs=[pl.BlockSpec(memory_space=pltpu.V...  52.4 us
    pallas_call x1, Pallas kernels, scattered_rows(): pl.pallas_call(scatter_kernel, in_specs=[pl.BlockSpec(memory_space=pltpu....  37 us
    pallas_call x1, Pallas kernels, project(): pl.pallas_call(functools.partial(project_kernel, strides), grid=(shards,)...  13.8 us
    pallas_call x1, Pallas kernels, compact_hidden(): pl.pallas_call(functools.partial(hidden_kernel, per_token), grid=(per_tok...  11.2 us
    psum x1, blocking collectives, per_device(): lax.psum(jnp.sum(embed_values * embed_values, axis=-1), 'tensor')  5.76 us

profile of v4, /device:TPU:0, one launch (start us, length us, event | category | flops | bytes accessed | tf_op | source)
XLA Modules:
  0.0 140.5 jit_solution(16258685578307755113)
XLA Ops:
  0.7 0.8 slice_multiply_fusion
  1.4 0.7 select_reduce_fusion.1
  2.1 0.6 slice.117
  2.7 0.6 reduce_max.18
  3.4 0.1 slice_bitcast_fusion.6
  3.4 0.7 fusion.19
  4.2 0.1 slice_bitcast_fusion.8
  4.2 1.4 %fusion.20 = (s32[]{:T(128)}, s32[8]{0:T(128)S(1)}, s32[8,1]{0,1:T(1,128)S(1)}) fusion(s32[5]{0:T(128)S(1)} %slice_bitcast_fusion.5, s32[3]{0:T(128)S(1)} %slice_bitcast_fusion.6, s32[6]{0:T(128)S(1)} %slice_bitcast_fusion.7, s32[2]{0:T(128)S(1)} %slice_bitcast_fusion.8, s32[7]{0:T(128)S(1)} %slice_bitcast_fusion.9, s32[1]{0:T(128)} %bitcast.8, ...), kind=kLoop, calls=%fused_computation.72 | loop fusion | flops 55 | bytes 196 | tf_op jit(solution)/shard_map/reduce_max | solution.py:401
  7.0 0.2 multiply_reduce_fusion.3
  7.2 0.6 dynamic_slice.14
  7.8 0.6 iota_compare_fusion.2
  8.5 0.1 multiply_reduce_fusion.2
  8.6 0.6 slice.130
  9.2 0.2 dynamic-slice_reduce_fusion.1
  9.3 0.1 select_reduce_fusion.3
  9.4 0.1 slice_bitcast_fusion.1
  9.5 0.1 add_bitcast_fusion.4
  9.6 0.1 slice_bitcast_fusion.3
  9.7 0.7 add_bitcast_fusion.2
  10.4 0.1 mul.95
  10.5 0.8 copy.52.index_ref
  11.3 0.0 copy-start
  11.3 11.2 %compact_hidden.1 = bf16[256,1280]{1,0:T(8,128)(2,1)S(1)} custom-call(bf16[1024,1280]{1,0:T(8,128)(2,1)} %patches_ref.1, f32[1280]{0:T(1024)} %gain_ref.1, f32[1280]{0:T(1024)} %bias_ref.1, bf16[5120,1280]{1,0:T(8,128)(2,1)} %weight_ref.1, f32[1280]{0:T(1024)} %first_bias_ref.1, s32[256,1]{1,0:T(8,128)} %copy.52.index_ref), custom_call_target="tpu_custom_call" | custom-call | flops 3355443200 | bytes 13107200 | tf_op jit(solution)/shard_map/compact_hidden/pallas_call | solution.py:54
  22.5 0.0 copy-done
  22.6 0.0 copy-start.3
  22.6 107.8 %conditional.6 = (bf16[256,2048]{1,0:T(8,128)(2,1)S(1)}) conditional(s32[]{:T(128)} %convert_element_type.37, (bf16[256,1280]{1,0:T(8,128)(2,1)S(1)}, s32[256]{0:T(256)S(1)}, s32[8,4]{0,1:T(4,128)S(1)}, s32[8,4,4]{0,2,1:T(4,128)S(1)}, s32[4]{0:T(128)S(1)}, /*index=5*/s32[8,4]{0,1:T(4,128)S(1)}, bf16[1280,1024]{1,0:T(8,128)(2,1)S(1)}) %tuple.36, ...), branch_computations={%region_7.10_spmd, %region_10.13_spmd} | conditional | flops 5368775168 | bytes 14723512
  22.6 0.8 slice.84.own_ref
  23.4 0.1 broadcast_add_fusion.1
  23.5 0.1 fusion.6
  23.6 1.2 copy.50.refs_4_
  24.8 52.4 %gather_rows.3.refs_0_.refs_1_.refs_2_.refs_3_ = bf16[8,192,1280]{2,1,0:T(8,128)(2,1)} custom-call(bf16[192,1280]{1,0:T(8,128)(2,1)} %slice.84.own_ref), custom_call_target="tpu_custom_call" | custom-call | tf_op jit(solution)/shard_map/cond/branch_1_fun/gather_rows/pallas_call | solution.py:189
  77.2 13.8 %project.3 = bf16[8,192,1024]{2,1,0:T(8,128)(2,1)} custom-call(bf16[8,192,1280]{2,1,0:T(8,128)(2,1)} %gather_rows.3.refs_0_.refs_1_.refs_2_.refs_3_, bf16[8,192,1280]{2,1,0:T(8,128)(2,1)} %gather_rows.3.refs_0_.refs_1_.refs_2_.refs_3_, bf16[8,192,1280]{2,1,0:T(8,128)(2,1)} %gather_rows.3.refs_0_.refs_1_.refs_2_.refs_3_, ...), custom_call_target="tpu_custom_call" | custom-call | flops 4026531840 | bytes 7864320 | tf_op jit(solution)/shard_map/cond/branch_1_fun/project/pallas_call | solution.py:96
  91.1 37.0 %scatter_rows.3 = bf16[4,2,48,1024]{3,2,1,0:T(8,128)(2,1)} custom-call(bf16[8,4,48,1024]{3,2,1,0:T(8,128)(2,1)} %bitcast.60), custom_call_target="tpu_custom_call" | custom-call | tf_op jit(solution)/shard_map/cond/branch_1_fun/scatter_rows/pallas_call | solution.py:351
  128.1 1.9 %copy.51 = bf16[4,48,2,1024]{3,2,1,0:T(2,128)(2,1)S(1)} copy(bf16[4,48,2,1024]{3,1,2,0:T(8,128)(2,1)} %bitcast.66) | data formatting | bytes 1572864 | tf_op jit(solution)/shard_map/cond/branch_1_fun/transpose | solution.py:366
  130.1 0.2 copy.54
  130.3 0.1 pad.6
  130.4 0.0 copy-done.3
  130.4 0.0 copy-start.2
  130.4 0.2 add_convert_fusion
  130.6 1.4 copy-done.2
  132.0 0.0 copy-start.4
  132.0 0.8 fusion.8
  132.8 0.0 copy-start.1
  132.8 5.8 %psum.7 = f32[512]{0:T(512)S(1)} all-reduce(f32[512]{0:T(512)S(1)} %get-tuple-element.66), channel_id=1, replica_groups=mesh['dp'=8,'tensor'=4] {'tensor'}, use_global_device_ids=true, to_apply=%region_14.15 | all-reduce | flops 512 | bytes 4096 | tf_op jit(solution)/shard_map/psum | solution.py:433
  138.6 0.0 copy-done.4
  138.6 1.9 %fusion.10 = bf16[512,2048]{1,0:T(8,128)(2,1)} fusion(bf16[512,2048]{1,0:T(8,128)(2,1)S(1)} %get-tuple-element.67, f32[2048]{0:T(1024)S(1)} %copy-done.4, f32[512]{0:T(512)S(1)} %add_rsqrt_fusion), kind=kLoop, calls=%fused_computation.26 | loop fusion | flops 4194304 | bytes 4204544 | tf_op jit(solution)/shard_map/convert_element_type | solution.py:435
  140.5 0.0 copy-done.1
  (18 shorter events, 0.1 us)
Async XLA Ops:
  11.3 11.2 %copy-start = (bf16[1280,1024]{1,0:T(8,128)(2,1)S(1)}, bf16[1280,1024]{1,0:T(8,128)(2,1)}, u32[]{:S(2)}) copy-start(bf16[1280,1024]{1,0:T(8,128)(2,1)} %param.18) | copy-start | bytes 7864324
  22.6 107.8 %copy-start.3 = (f32[2048]{0:T(1024)S(1)}, f32[2048]{0:T(1024)}, u32[]{:S(2)}) copy-start(f32[2048]{0:T(1024)} %param.19) | copy-start | bytes 24580
  130.4 1.6 %copy-start.2 = (bf16[512,2048]{1,0:T(8,128)(2,1)S(1)}, bf16[512,2048]{1,0:T(8,128)(2,1)}, u32[]{:S(2)}) copy-start(bf16[512,2048]{1,0:T(8,128)(2,1)} %param.20) | copy-start | bytes 6291460
  132.0 6.6 %copy-start.4 = (f32[2048]{0:T(1024)S(1)}, f32[2048]{0:T(1024)}, u32[]{:S(2)}) copy-start(f32[2048]{0:T(1024)} %param.21) | copy-start | bytes 24580
  132.8 7.7 %copy-start.1 = (bf16[512,2048]{1,0:T(8,128)(2,1)}, bf16[512,2048]{1,0:T(8,128)(2,1)S(1)}, u32[]{:S(2)}) copy-start(bf16[512,2048]{1,0:T(8,128)(2,1)S(1)} %get-tuple-element.67) | copy-start | bytes 6291460
